TPU v7x, 512 devices: a 8x2x16 block of a 8x8x16 slice. The times are simulated.
512 devices in a mesh: groups: 2 (over y), batch: 16 (over z), blk: 16 (over x, core).
Axes of the slice: x: 8, y: 2, z: 16, core: 2. Of those that a mesh axis runs over, the one named last changes fastest.
The devices are a block of a 8x8x16 slice.
Arguments:
- queries: bfloat16 [32, 2368, 1024], P(('groups', 'batch'), 'blk'), parts along dimension 0, may hold values from -12 to 12
- key_states: bfloat16 [32, 2368, 1024], P(('groups', 'batch'), 'blk'), parts along dimension 0, may hold values from -6 to 6
- value_states: bfloat16 [32, 2368, 1024], P(('groups', 'batch'), 'blk'), parts along dimension 0, may hold values from -6 to 6
- residual: bfloat16 [32, 2368, 768], P(('groups', 'batch'), 'blk'), parts along dimension 0, may hold values from -3 to 3
- proj_weight: bfloat16 [1024, 768], P(None, 'batch'), may hold values from -0.1875 to 0.1875
- conv_weight: bfloat16 [3, 3, 768, 384], P(None, None, 'batch'), may hold values from -0.078125 to 0.078125
Outputs:
- conv_out: bfloat16 [32, 2368, 384], P(('groups', 'batch'), 'blk'), parts along dimension 0
There are 2 independent parts, one for each index of `groups`. A program takes and returns all parts, laid end to end along the dimension named above; an argument that names none is the same for every part. Nothing has to cross between parts.
All inputs are finite; a program needn't handle non-finite values.
Results may differ from a plain program's by a relative error of at most 0.0085.
Values may be sent and summed in bfloat16 or wider, within the bound.
A program may use at most 64 MiB of HBM per device.

v0:
```python
import jax
import jax.numpy as jnp
from jax import lax
from jax.sharding import PartitionSpec as P

HEADS = 16
HD = 64
COLS = 74
ROWS = 2


def extended(cells, sides, width):
    for axis, dim in sides:
        count = lax.axis_size(axis)
        ends = count - 1
        head = lax.slice_in_dim(cells, 0, width, axis=dim)
        tail = lax.slice_in_dim(cells, cells.shape[dim] - width, cells.shape[dim], axis=dim)
        cells = jnp.concatenate(
            [
                lax.ppermute(tail, axis, [(i, (i + 1) % count) for i in range(ends)]),
                cells,
                lax.ppermute(head, axis, [((i + 1) % count, i) for i in range(ends)]),
            ],
            axis=dim,
        )
    return cells


def empty_state(head_count, query_rows):
    return (
        jnp.full((head_count, query_rows), -1e30, jnp.float32),
        jnp.zeros((head_count, query_rows), jnp.float32),
        jnp.zeros((head_count, query_rows, HD), jnp.float32),
    )


def absorb(carry_state, query_block, key_block, value_block):
    row_max, weight_sum, running = carry_state
    scores = jnp.einsum(
        "qhd,khd->hqk", query_block, key_block, preferred_element_type=jnp.float32
    ) * HD ** (-0.5)
    new_max = jnp.maximum(row_max, jnp.max(scores, axis=2))
    factor = jnp.exp(row_max - new_max)
    weights = jnp.exp(scores - new_max[:, :, None])
    weight_sum = weight_sum * factor + jnp.sum(weights, axis=2)
    running = running * factor[:, :, None] + jnp.einsum(
        "hqk,khd->hqd",
        weights.astype(jnp.bfloat16),
        value_block,
        preferred_element_type=jnp.float32,
    )
    return (new_max, weight_sum, running)


def finish(carry_state):
    row_max, weight_sum, running = carry_state
    mixed = running / weight_sum[:, :, None]
    head_count, query_rows = weight_sum.shape
    return mixed.transpose(1, 0, 2).reshape(query_rows, head_count * HD).astype(jnp.bfloat16)


def body(queries, key_states, value_states, residual, proj_weight, conv_weight):
    query_rows = queries[0]
    key_rows = key_states[0]
    value_rows = value_states[0]
    tok_rows = query_rows.shape[0]
    cycle_count = lax.axis_size("blk")
    local_heads = HEADS // cycle_count
    query_all, key_all, value_all = (
        lax.all_to_all(query_rows, "blk", split_axis=1, concat_axis=0, tiled=True),
        lax.all_to_all(key_rows, "blk", split_axis=1, concat_axis=0, tiled=True),
        lax.all_to_all(value_rows, "blk", split_axis=1, concat_axis=0, tiled=True),
    )
    seq_rows = tok_rows * cycle_count
    group = 1
    while cycle_count % (group * 2) == 0 and tok_rows * group * 2 <= 1024:
        group = group * 2
    block_rows = tok_rows * group
    block_count = seq_rows // block_rows
    query_blocks = query_all.reshape(block_count, block_rows, local_heads, HD)
    key_blocks = key_all.reshape(block_count, block_rows, local_heads, HD)
    value_blocks = value_all.reshape(block_count, block_rows, local_heads, HD)

    def one_block(query_block):

        def absorb_one(index, inner_state):
            return absorb(inner_state, query_block, key_blocks[index], value_blocks[index])

        return finish(
            lax.fori_loop(0, block_count, absorb_one, empty_state(local_heads, block_rows))
        )

    mixed_rows = lax.map(one_block, query_blocks).reshape(seq_rows, local_heads * HD)
    attention = lax.all_to_all(mixed_rows, "blk", split_axis=0, concat_axis=1, tiled=True)
    projected = jnp.dot(
        attention,
        lax.all_gather(proj_weight, "batch", axis=1, tiled=True),
        preferred_element_type=jnp.float32,
    )
    hidden = (residual[0].astype(jnp.float32) + projected).astype(jnp.bfloat16)
    feature_grid = hidden.reshape(ROWS, COLS, hidden.shape[1])
    rimmed = extended(feature_grid, (("blk", 0),), 1)
    padded = jnp.pad(rimmed, ((0, 0), (1, 1), (0, 0)))
    shard_piece = lax.all_gather(conv_weight, "batch", axis=2, tiled=True)
    piece_rows = shard_piece.shape[2]
    windows = []
    for row_off in range(3):
        for col_off in range(3):
            windows.append(
                padded[row_off : row_off + ROWS, col_off : col_off + COLS].reshape(
                    tok_rows, piece_rows
                )
            )
    stacked = jnp.concatenate(windows, axis=1)
    flat_weight = shard_piece.reshape(9 * piece_rows, shard_piece.shape[3])
    conv_sum = jnp.dot(stacked, flat_weight, preferred_element_type=jnp.float32)
    return conv_sum.astype(jnp.bfloat16)[None]


def solution(mesh):
    return jax.shard_map(
        body,
        mesh=mesh,
        in_specs=(
            P(("groups", "batch"), "blk", None),
            P(("groups", "batch"), "blk", None),
            P(("groups", "batch"), "blk", None),
            P(("groups", "batch"), "blk", None),
            P(None, "batch"),
            P(None, None, "batch", None),
        ),
        out_specs=P(("groups", "batch"), "blk", None),
        check_vma=False,
    )
```

profile of v0, /device:TPU:66, one launch (start us, length us, event | category | flops | bytes accessed | tf_op | source)
XLA Modules:
  0.0 209.9 jit_solution(13141760335424356160)
XLA Ops:
  7.3 2.0 copy.30
  9.3 43.8 %all-to-all-start = ((bf16[148,16,64]{0,2,1:T(8,128)(2,1)}), bf16[148,16,64]{0,2,1:T(8,128)(2,1)S(1)}, u32[]{:S(2)}, u32[]{:S(2)}) async-start(bf16[148,16,64]{0,2,1:T(8,128)(2,1)} %bitcast.2), calls=%async_computation | async-start | bytes 1048576 | tf_op jit(solution)/shard_map/all_to_all | solution.py:70
  53.1 1.0 copy.31
  54.1 13.1 %all-to-all-done = bf16[148,16,64]{0,2,1:T(8,128)(2,1)S(1)} async-done(((bf16[148,16,64]{0,2,1:T(8,128)(2,1)}), bf16[148,16,64]{0,2,1:T(8,128)(2,1)S(1)}, u32[]{:S(2)}, u32[]{:S(2)}) %all-to-all-start) | async-done | bytes 303136 | tf_op jit(solution)/shard_map/all_to_all | solution.py:70
  67.1 6.3 %all-to-all-start.1 = ((bf16[148,16,64]{0,2,1:T(8,128)(2,1)}), bf16[148,16,64]{0,2,1:T(8,128)(2,1)S(1)}, u32[]{:S(2)}, u32[]{:S(2)}) async-start(bf16[148,16,64]{0,2,1:T(8,128)(2,1)} %bitcast.4), calls=%async_computation.1 | async-start | bytes 1048576 | tf_op jit(solution)/shard_map/all_to_all | solution.py:71
  73.4 1.0 copy.32
  74.4 13.5 %all-to-all-done.1 = bf16[148,16,64]{0,2,1:T(8,128)(2,1)S(1)} async-done(((bf16[148,16,64]{0,2,1:T(8,128)(2,1)}), bf16[148,16,64]{0,2,1:T(8,128)(2,1)S(1)}, u32[]{:S(2)}, u32[]{:S(2)}) %all-to-all-start.1) | async-done | bytes 303136 | tf_op jit(solution)/shard_map/all_to_all | solution.py:71
  87.9 5.7 %all-to-all-start.2 = ((bf16[148,16,64]{0,2,1:T(8,128)(2,1)}), bf16[148,16,64]{0,2,1:T(8,128)(2,1)S(1)}, u32[]{:S(2)}, u32[]{:S(2)}) async-start(bf16[148,16,64]{0,2,1:T(8,128)(2,1)} %bitcast.6), calls=%async_computation.2 | async-start | bytes 1048576 | tf_op jit(solution)/shard_map/all_to_all | solution.py:72
  96.7 11.3 %all-to-all-done.2 = bf16[148,16,64]{0,2,1:T(8,128)(2,1)S(1)} async-done(((bf16[148,16,64]{0,2,1:T(8,128)(2,1)}), bf16[148,16,64]{0,2,1:T(8,128)(2,1)S(1)}, u32[]{:S(2)}, u32[]{:S(2)}) %all-to-all-start.2) | async-done | bytes 303136 | tf_op jit(solution)/shard_map/all_to_all | solution.py:72
  109.2 19.2 %while.29 = (s32[]{:T(128)}, bf16[4,592,64]{1,2,0:T(8,128)(2,1)S(1)}, bf16[4,592,1,64]{1,3,2,0:T(8,128)(2,1)S(1)}, bf16[4,592,1,64]{1,3,2,0:T(8,128)(2,1)S(1)}, ...) while((s32[]{:T(128)}, ...), condition=%wide.region_5.6_spmd, body=%wide.region_0.5_spmd.sunk | while | flops 92014560 | bytes 5330546 | solution.py:93
  109.3 4.7 %while.30 = (s32[]{:T(128)}, f32[1,592]{1,0:T(1,128)S(1)}, f32[1,592]{1,0:T(1,128)S(1)}, f32[1,592,64]{1,2,0:T(8,128)S(1)}, bf16[4,592,1,64]{1,3,2,0:T(8,128)(2,...) while((s32[]{:T(128)}, f32[1,592]{1,0:T(1,128)S(1)}, ...), condition=%wide.region_4.4_spmd.clone, body=%wide.region_1.3_spmd.clone.sunk | while | flops 91938784 | bytes 4924209 | solution.py:90
  114.1 4.7 %while.30 = (s32[]{:T(128)}, f32[1,592]{1,0:T(1,128)S(1)}, f32[1,592]{1,0:T(1,128)S(1)}, f32[1,592,64]{1,2,0:T(8,128)S(1)}, bf16[4,592,1,64]{1,3,2,0:T(8,128)(2,...) while((s32[]{:T(128)}, f32[1,592]{1,0:T(1,128)S(1)}, ...), condition=%wide.region_4.4_spmd.clone, body=%wide.region_1.3_spmd.clone.sunk | while | flops 91938784 | bytes 4924209 | solution.py:90
  118.9 4.7 %while.30 = (s32[]{:T(128)}, f32[1,592]{1,0:T(1,128)S(1)}, f32[1,592]{1,0:T(1,128)S(1)}, f32[1,592,64]{1,2,0:T(8,128)S(1)}, bf16[4,592,1,64]{1,3,2,0:T(8,128)(2,...) while((s32[]{:T(128)}, f32[1,592]{1,0:T(1,128)S(1)}, ...), condition=%wide.region_4.4_spmd.clone, body=%wide.region_1.3_spmd.clone.sunk | while | flops 91938784 | bytes 4924209 | solution.py:90
  123.7 4.7 %while.30 = (s32[]{:T(128)}, f32[1,592]{1,0:T(1,128)S(1)}, f32[1,592]{1,0:T(1,128)S(1)}, f32[1,592,64]{1,2,0:T(8,128)S(1)}, bf16[4,592,1,64]{1,3,2,0:T(8,128)(2,...) while((s32[]{:T(128)}, f32[1,592]{1,0:T(1,128)S(1)}, ...), condition=%wide.region_4.4_spmd.clone, body=%wide.region_1.3_spmd.clone.sunk | while | flops 91938784 | bytes 4924209 | solution.py:90
  129.4 19.8 %all_to_all.67 = bf16[16,148,64]{1,2,0:T(8,128)(2,1)S(1)} all-to-all(bf16[16,148,64]{1,2,0:T(8,128)(2,1)S(1)} %copy.28), channel_id=1, replica_groups=mesh['groups'=2,'batch'=16,'blk'=16] {'blk'}, dimensions={0} | all-to-all | bytes 606208 | tf_op jit(solution)/shard_map/all_to_all | solution.py:94
  149.2 2.1 %fusion.16 = bf16[148,768]{1,0:T(8,128)(2,1)S(1)} fusion(bf16[148,1024]{0,1:T(8,128)(2,1)S(1)} %bitcast.61, bf16[1024,768]{0,1:T(8,128)(2,1)} %all-gather.3.cloned.1.call-done, bf16[1,148,768]{2,1,0:T(8,128)(2,1)S(1)} %copy-done.2), kind=kOutput, calls=%fused_computation.28 | convolution fusion | flops 233124864 | bytes 2330624 | tf_op jit(solution)/shard_map/dot_general | solution.py:95
  151.4 2.4 %collective-permute-start = (bf16[1,74,768]{2,1,0:T(8,128)(2,1)S(1)}, bf16[1,74,768]{2,1,0:T(8,128)(2,1)S(1)}, u32[]{:S(2)}, u32[]{:S(2)}) collective-permute-start(bf16[1,74,768]{2,1,0:T(8,128)(2,1)S(1)} %get-tuple-element.229), channel_id=1, source_target_pairs={{0,1},{1,2},{2,3},{3,4},{4,5},{5,6},{6,7},{7,8},{8,9},{9,10},{10,1... | collective-permute-start | bytes 341000 | tf_op jit(solution)/shard_map/ppermute | solution.py:20
  153.7 4.6 %collective-permute-start.1 = (bf16[1,74,768]{2,1,0:T(8,128)(2,1)S(1)}, bf16[1,74,768]{2,1,0:T(8,128)(2,1)S(1)}, u32[]{:S(2)}, u32[]{:S(2)}) collective-permute-start(bf16[1,74,768]{2,1,0:T(8,128)(2,1)S(1)} %get-tuple-element.230), channel_id=1, source_target_pairs={{1,0},{2,1},{3,2},{4,3},{5,4},{6,5},{7,6},{8,7},{9,8},{10,9},{11,1... | collective-permute-start | bytes 341000 | tf_op jit(solution)/shard_map/ppermute | solution.py:22
  159.0 1.8 collective-permute-done.1
  163.7 1.0 constant_dynamic-update-slice_fusion.7
  164.7 1.0 constant_dynamic-update-slice_fusion.6
  165.6 1.0 constant_dynamic-update-slice_fusion.5
  166.7 31.8 %all-gather.5.cloned.1.call-done = bf16[3,3,768,384]{3,2,1,0:T(8,128)(2,1)} async-done(((bf16[3,3,48,384]{3,2,1,0:T(8,128)(2,1)}), bf16[3,3,768,384]{3,2,1,0:T(8,128)(2,1)}) %all-gather.5.cloned.1.call-update) | async-done | bytes 5308432 | tf_op jit(solution)/shard_map/all_gather | solution.py:104
  198.6 4.5 %fusion.17 = bf16[1,148,384]{2,1,0:T(8,128)(2,1)} fusion(bf16[148,6912]{1,0:T(8,128)(2,1)S(1)} %constant_dynamic-update-slice_fusion, bf16[6912,384]{1,0:T(8,128)(2,1)} %bitcast.60), kind=kOutput, calls=%fused_computation.30 | convolution fusion | flops 785702400 | bytes 7468032 | tf_op jit(solution)/shard_map/dot_general | solution.py:116
  (164 shorter events, 27.7 us)
Async XLA Ops:
  6.5 46.5 %copy-start = (bf16[1,148,1024]{2,1,0:T(8,128)(2,1)S(1)}, bf16[1,148,1024]{2,1,0:T(8,128)(2,1)}, u32[]{:S(2)}) copy-start(bf16[1,148,1024]{2,1,0:T(8,128)(2,1)} %param.11) | copy-start | bytes 909316
  6.5 66.9 %copy-start.1 = (bf16[1,148,1024]{2,1,0:T(8,128)(2,1)S(1)}, bf16[1,148,1024]{2,1,0:T(8,128)(2,1)}, u32[]{:S(2)}) copy-start(bf16[1,148,1024]{2,1,0:T(8,128)(2,1)} %param.12) | copy-start | bytes 909316
  6.6 142.7 %all-gather.3.cloned.1.call-start = ((), (), s32[]{:S(2)}) async-start(), calls=%async_computation.4 | async-start | bytes 1671168 | tf_op jit(solution)/shard_map/all_gather | solution.py:97
  9.3 57.9 %all-to-all-start = ((bf16[148,16,64]{0,2,1:T(8,128)(2,1)}), bf16[148,16,64]{0,2,1:T(8,128)(2,1)S(1)}, u32[]{:S(2)}, u32[]{:S(2)}) async-start(bf16[148,16,64]{0,2,1:T(8,128)(2,1)} %bitcast.2), calls=%async_computation | async-start | bytes 1048576 | tf_op jit(solution)/shard_map/all_to_all | solution.py:70
  67.1 20.7 %all-to-all-start.1 = ((bf16[148,16,64]{0,2,1:T(8,128)(2,1)}), bf16[148,16,64]{0,2,1:T(8,128)(2,1)S(1)}, u32[]{:S(2)}, u32[]{:S(2)}) async-start(bf16[148,16,64]{0,2,1:T(8,128)(2,1)} %bitcast.4), calls=%async_computation.1 | async-start | bytes 1048576 | tf_op jit(solution)/shard_map/all_to_all | solution.py:71
  87.9 20.2 %all-to-all-start.2 = ((bf16[148,16,64]{0,2,1:T(8,128)(2,1)}), bf16[148,16,64]{0,2,1:T(8,128)(2,1)S(1)}, u32[]{:S(2)}, u32[]{:S(2)}) async-start(bf16[148,16,64]{0,2,1:T(8,128)(2,1)} %bitcast.6), calls=%async_computation.2 | async-start | bytes 1048576 | tf_op jit(solution)/shard_map/all_to_all | solution.py:72
  93.6 105.0 %all-gather.5.cloned.1.call-start = ((), (), s32[]{:S(2)}) async-start(), calls=%async_computation.5 | async-start | bytes 5640192 | tf_op jit(solution)/shard_map/all_gather | solution.py:104
  128.5 20.8 %copy-start.2 = (bf16[1,148,768]{2,1,0:T(8,128)(2,1)S(1)}, bf16[1,148,768]{2,1,0:T(8,128)(2,1)}, u32[]{:S(2)}) copy-start(bf16[1,148,768]{2,1,0:T(8,128)(2,1)} %param.13) | copy-start | bytes 681988
  151.4 7.6 %collective-permute-start = (bf16[1,74,768]{2,1,0:T(8,128)(2,1)S(1)}, bf16[1,74,768]{2,1,0:T(8,128)(2,1)S(1)}, u32[]{:S(2)}, u32[]{:S(2)}) collective-permute-start(bf16[1,74,768]{2,1,0:T(8,128)(2,1)S(1)} %get-tuple-element.229), channel_id=1, source_target_pairs={{0,1},{1,2},{2,3},{3,4},{4,5},{5,6},{6,7},{7,8},{8,9},{9,10},{10,1... | collective-permute-start | bytes 341000 | tf_op jit(solution)/shard_map/ppermute | solution.py:20
  153.7 7.1 %collective-permute-start.1 = (bf16[1,74,768]{2,1,0:T(8,128)(2,1)S(1)}, bf16[1,74,768]{2,1,0:T(8,128)(2,1)S(1)}, u32[]{:S(2)}, u32[]{:S(2)}) collective-permute-start(bf16[1,74,768]{2,1,0:T(8,128)(2,1)S(1)} %get-tuple-element.230), channel_id=1, source_target_pairs={{1,0},{2,1},{3,2},{4,3},{5,4},{6,5},{7,6},{8,7},{9,8},{10,9},{11,1... | collective-permute-start | bytes 341000 | tf_op jit(solution)/shard_map/ppermute | solution.py:22
Sparse Core Ops, SparseCore 0:
  9.4 107.5 all-gather.2
  119.1 79.3 all-gather.4
where the time goes:
time: 211 us; the launch traced here: 210 us
  waiting for transfers between devices  73.5 us (35%)
  starting transfers between devices  62.9 us (30%)
  matrix products  19.8 us (9%)
  blocking collectives  19.8 us (9%)
  local copies, waits for them, and re-layouts  14.1 us (7%)
  between operations  13.7 us (6%)
  other arithmetic  5.1 us (2%)
    all_to_all x1, starting transfers between devices, body(): lax.all_to_all(query_rows, 'blk', split_axis=1, concat_axis=0, tiled=True)  43.8 us
    all_gather x1, waiting for transfers between devices, body(): shard_piece = lax.all_gather(conv_weight, 'batch', axis=2, tiled=True)  31.8 us
    all_to_all x1, blocking collectives, body(): lax.all_to_all(mixed_rows, 'blk', split_axis=0, concat_axis=1, tiled=True)  19.8 us
    all_to_all x1, waiting for transfers between devices, body(): lax.all_to_all(key_rows, 'blk', split_axis=1, concat_axis=0, tiled=True)  13.5 us
    all_to_all x1, waiting for transfers between devices, body(): lax.all_to_all(query_rows, 'blk', split_axis=1, concat_axis=0, tiled=True)  13.1 us
    all_to_all x1, waiting for transfers between devices, body(): lax.all_to_all(value_rows, 'blk', split_axis=1, concat_axis=0, tiled=True)  11.3 us
    dot_general x16, matrix products, absorb(): jnp.einsum('qhd,khd->hqk', query_block, key_block, preferred_element_type...  7.06 us
    all_to_all x1, starting transfers between devices, body(): lax.all_to_all(key_rows, 'blk', split_axis=1, concat_axis=0, tiled=True)  6.27 us
  transfers between devices with their start and end apart: 7, of which 6 were waited for; matrix products, arithmetic and copies ran while one was open for 16% of the time, Pallas kernels for 0%

commit v1 on v0

v1 whole, which is shorter than its diff:
```python
import functools

import jax
import jax.numpy as jnp
from jax import lax
from jax.experimental import pallas as pl
from jax.experimental.pallas import tpu as pltpu
from jax.sharding import PartitionSpec as P

HD = 64
COLS = 74
ROWS = 2
LANES = 128
LOG2E = 1.4426950408889634
MESH = pl.DeviceIdType.MESH
F32 = jnp.float32
BF16 = jnp.bfloat16
NT = (((1,), (1,)), ((), ()))


def up16(n):
    return -(-n // 16) * 16


def one_hot(rows, depth, dc, pitch, flag):
    i = lax.broadcasted_iota(jnp.int32, (rows, depth), 0)
    t = lax.broadcasted_iota(jnp.int32, (rows, depth), 1)
    r = jnp.where(i >= pitch, 1, 0)
    c = i - r * pitch
    src = c + (dc - 1)
    ok = (t == r * COLS + src) & (c < COLS) & (src >= 0) & (src < COLS)
    if flag is not None:
        ok = ok & flag
    return jnp.where(ok, 1.0, 0.0).astype(BF16)


def kernel(dims, q, k, v, res, w, out, kin, vin, qin, ob, ain, wall, kpad, vaug, qpad,
           hpad, grid, hin, rbuf, k_s, k_r, v_s, v_r, q_s, q_r, o_s, o_r, kf_s, kf_r,
           vf_s, vf_r, w_s, w_r, p_s, p_r, h_s, h_r, loc):
    nb, nz, tok, slab, taps, pitch, cp = dims
    xn = nb // 2
    half = taps // 2
    blk = lax.axis_index("blk")
    z = lax.axis_index("batch")
    x = blk // 2
    c = blk % 2
    mate = 2 * x + 1 - c
    side = lax.rem(blk + nb + 2 * c - 1, nb)
    znext = (lax.rem(z + 1, nz), lax.rem(z + nz - 1, nz))
    hops = (nz // 2, nz - 1 - nz // 2)

    def at_x(i):
        off = ((i + 1) // 2) * (2 * (i % 2) - 1)
        return lax.rem(x + off + xn, xn)

    def wait(ref, sem):
        pltpu.make_async_copy(ref, ref, sem).wait()

    def send(src, dst, s_sem, r_sem, **where):
        pltpu.make_async_remote_copy(
            src_ref=src, dst_ref=dst, send_sem=s_sem, recv_sem=r_sem,
            device_id=where, device_id_type=MESH,
        ).start()

    barrier = pltpu.get_barrier_semaphore()
    for i in range(1, xn):
        pl.semaphore_signal(barrier, inc=1, device_id={"blk": 2 * at_x(i) + c}, device_id_type=MESH)
    for b in (mate, side):
        pl.semaphore_signal(barrier, inc=1, device_id={"blk": b}, device_id_type=MESH)
    for n in znext:
        pl.semaphore_signal(barrier, inc=1, device_id={"batch": n}, device_id_type=MESH)
    pl.semaphore_wait(barrier, xn - 1 + 4)

    def cols(i):
        return pl.ds(pl.multiple_of(i * LANES, LANES), LANES)

    def slab_rows(zz):
        return pl.ds(pl.multiple_of(zz * slab, slab), slab)

    for i in range(1, xn):
        d = at_x(i)
        send(k.at[0, :, cols(d)], kin.at[c, x], k_s.at[i], k_r.at[x], blk=2 * d + c)
        send(v.at[0, :, cols(d)], vin.at[c, x], v_s.at[i], v_r.at[x], blk=2 * d + c)
        if i == 2:
            for j in range(half):
                for way in range(2):
                    send(w.at[half * c + j], wall.at[half * c + j, slab_rows(z)],
                         w_s.at[way, j], w_r.at[way, 0, j], batch=znext[way])
    for i in range(1, xn):
        d = at_x(i)
        send(q.at[0, :, cols(d)], qin.at[x], q_s.at[i], q_r.at[x], blk=2 * d + c)
    pltpu.make_async_copy(k.at[0, :, cols(x)], kin.at[c, x], k_r.at[x]).start()
    pltpu.make_async_copy(v.at[0, :, cols(x)], vin.at[c, x], v_r.at[x]).start()
    pltpu.make_async_copy(q.at[0, :, cols(x)], qin.at[x], q_r.at[x]).start()
    pltpu.make_async_copy(w, wall.at[:, slab_rows(z)], loc.at[0]).start()
    pltpu.make_async_copy(res.at[0], rbuf, loc.at[1]).start()

    def tick(t, carry):
        s = t // half
        j = lax.rem(t, half)
        for way in range(2):
            zz = lax.rem(z + (1 + s if way else 2 * nz - 1 - s), nz)

            def work():
                ref = wall.at[half * c + j, slab_rows(zz)]
                wait(ref, w_r.at[way, s, j])

                @pl.when(s < hops[way] - 1)
                def _():
                    wait(ref, w_s.at[way, j])
                    send(ref, ref, w_s.at[way, j], w_r.at[way, s + 1, j], batch=znext[way])

                @pl.when(s > 0)
                def _():
                    wait(ref, p_s.at[way, j])

                send(ref, ref, p_s.at[way, j], p_r.at[way, s, j], blk=mate)

            if hops[way] == hops[0]:
                work()
            else:
                pl.when(s < hops[way])(work)
        return carry

    def ticks(lo, hi):
        lax.fori_loop(lo, hi, tick, 0)

    kpad[...] = jnp.zeros_like(kpad)
    vaug[...] = jnp.zeros_like(vaug)
    qpad[...] = jnp.zeros_like(qpad)
    hpad[...] = jnp.zeros_like(hpad)

    tail = tok // 16 * 16

    def place(p, xs):
        base = (p * xn + xs) * pitch
        kpad[pl.ds(pl.multiple_of(base, 16), tok), :] = kin[p, xs]
        last = kpad[pl.ds(pl.multiple_of(base + tail, 16), 16), :].astype(F32)
        prior = kpad[pl.ds(pl.multiple_of(base + tail - 16, 16), 16), :].astype(F32)
        row = lax.broadcasted_iota(jnp.int32, (16, LANES), 0)
        kpad[pl.ds(pl.multiple_of(base + tail, 16), 16), :] = jnp.where(
            row < tok - tail, last, prior).astype(BF16)
        vaug[pl.ds(pl.multiple_of(base, 16), tok), 0:LANES] = vin[p, xs]
        vaug[pl.ds(pl.multiple_of(base, 16), tok), LANES:2 * LANES] = jnp.ones((tok, LANES), BF16)

    def take(i, carry):
        xs = at_x(i)
        wait(kin.at[c, xs], k_r.at[xs])
        send(kin.at[c, xs], kin.at[c, xs], kf_s.at[xs], kf_r.at[xs], blk=mate)
        wait(vin.at[c, xs], v_r.at[xs])
        send(vin.at[c, xs], vin.at[c, xs], vf_s.at[xs], vf_r.at[xs], blk=mate)
        place(c, xs)
        lax.fori_loop(2 * i, 2 * i + 2, tick, 0)
        return carry

    lax.fori_loop(0, xn, take, 0)

    def take_mate(i, carry):
        xs = at_x(i)
        wait(kin.at[1 - c, xs], kf_r.at[xs])
        wait(vin.at[1 - c, xs], vf_r.at[xs])
        place(1 - c, xs)
        return carry

    lax.fori_loop(0, xn, take_mate, 0)

    lane = lax.broadcasted_iota(jnp.int32, (tok, LANES), 1)
    scale = HD ** -0.5 * LOG2E

    def attend(i, carry):
        xs = at_x(i)
        wait(qin.at[xs], q_r.at[xs])
        qv = qin[xs].astype(F32)
        qpad[0:tok, :] = jnp.where(lane < HD, qv, 0.0).astype(BF16)
        qpad[pitch:pitch + tok, :] = jnp.where(lane < HD, 0.0, qv).astype(BF16)
        scores = lax.dot_general(qpad[...], kpad[...], NT, preferred_element_type=F32)
        top = jnp.max(scores, axis=1, keepdims=True)
        weights = jnp.exp2((scores - top) * scale).astype(BF16)
        mixed = jnp.dot(weights, vaug[...], preferred_element_type=F32)
        both = mixed[:, :LANES] / mixed[:, LANES:]
        ob[xs] = jnp.where(lane < HD, both[0:tok], both[pitch:pitch + tok]).astype(BF16)

        @pl.when(i == 0)
        def _():
            ain[x] = ob[x]

        @pl.when(i > 0)
        def _():
            send(ob.at[xs], ain.at[x], o_s.at[xs], o_r.at[x], blk=2 * xs + c)

        lax.fori_loop(2 * xn + 2 * i, 2 * xn + 2 * i + 2, tick, 0)
        return carry

    lax.fori_loop(0, xn, attend, 0)
    ticks(4 * xn, hops[0] * half)

    for way in range(2):
        for s in range(hops[way]):
            zz = lax.rem(z + (1 + s if way else 2 * nz - 1 - s), nz)
            for j in range(half):
                wait(wall.at[half * (1 - c) + j, slab_rows(zz)], p_r.at[way, s, j])
    wait(wall.at[:, slab_rows(z)], loc.at[0])
    wait(rbuf, loc.at[1])
    for i in range(1, xn):
        xs = at_x(i)
        wait(ain.at[xs], o_r.at[xs])

    attention = jnp.concatenate([ain[i] for i in range(xn)], axis=1)
    width = wall.shape[2]
    total = rbuf[...].astype(F32)
    convs = taps - (-(-attention.shape[1] // width))
    for b in range(convs, taps):
        lo = (b - convs) * width
        hi = min(lo + width, attention.shape[1])
        total = total + lax.dot_general(
            attention[:, lo:hi], wall[b, :, 0:hi - lo], NT, preferred_element_type=F32)
    hpad[0:tok, :] = total.astype(BF16)

    hid = hpad[...]
    for dc in (1, 0, 2):
        grid[dc, cp:3 * cp, :] = jnp.dot(
            one_hot(2 * cp, pitch, dc, cp, None), hid, preferred_element_type=F32).astype(BF16)
        if dc == 1:
            send(grid.at[1, cp:2 * cp], hin.at[1], h_s.at[0], h_r.at[1],
                 blk=lax.rem(blk + nb - 1, nb))
            send(grid.at[1, 2 * cp:3 * cp], hin.at[0], h_s.at[1], h_r.at[0],
                 blk=lax.rem(blk + 1, nb))

    both_rows = jnp.zeros((2 * cp, out.shape[1]), F32)
    for dc in range(3):
        both_rows += jnp.dot(grid[dc, cp:3 * cp, :], wall[3 + dc], preferred_element_type=F32)
    upper = both_rows[0:cp]
    lower = both_rows[cp:2 * cp]
    for dc in range(3):
        upper += jnp.dot(grid[dc, 2 * cp:3 * cp, :], wall[6 + dc], preferred_element_type=F32)
        lower += jnp.dot(grid[dc, cp:2 * cp, :], wall[dc], preferred_element_type=F32)
    wait(hin.at[0], h_r.at[0])
    wait(hin.at[1], h_r.at[1])
    for dc in range(3):
        above = jnp.dot(one_hot(cp, cp, dc, cp, blk > 0), hin[0], preferred_element_type=F32)
        below = jnp.dot(one_hot(cp, cp, dc, cp, blk < nb - 1), hin[1], preferred_element_type=F32)
        upper += jnp.dot(above.astype(BF16), wall[dc], preferred_element_type=F32)
        lower += jnp.dot(below.astype(BF16), wall[6 + dc], preferred_element_type=F32)
    out[0:cp, :] = upper.astype(BF16)
    out[cp:2 * cp, :] = lower.astype(BF16)

    for i in range(1, xn):
        xs = at_x(i)
        wait(kin.at[c, 0], k_s.at[i])
        wait(vin.at[c, 0], v_s.at[i])
        wait(qin.at[0], q_s.at[i])
        wait(ob.at[xs], o_s.at[xs])
    for i in range(xn):
        wait(kin.at[c, i], kf_s.at[i])
        wait(vin.at[c, i], vf_s.at[i])
    for way in range(2):
        for j in range(half):
            wait(wall.at[j, slab_rows(z)], w_s.at[way, j])
            wait(wall.at[j, slab_rows(z)], p_s.at[way, j])
    wait(hin.at[0], h_s.at[0])
    wait(hin.at[1], h_s.at[1])


def body(queries, key_states, value_states, residual, proj_weight, conv_weight):
    nb = lax.axis_size("blk")
    nz = lax.axis_size("batch")
    tok = queries.shape[1]
    slab = conv_weight.shape[2]
    width = conv_weight.shape[3]
    depth = proj_weight.shape[0]
    blocks = -(-depth // width)
    flat = jnp.pad(proj_weight, ((0, blocks * width - depth), (0, 0)))
    flat = flat.reshape(blocks, width, slab).transpose(0, 2, 1)
    weights = jnp.concatenate([conv_weight.reshape(9, slab, width), flat], axis=0)
    taps = weights.shape[0]
    half = taps // 2
    xn = nb // 2
    pitch = up16(tok)
    cp = up16(COLS)
    feats = nz * slab
    hops = nz // 2
    dma = pltpu.SemaphoreType.DMA
    any_space = pl.BlockSpec(memory_space=pl.ANY)
    got = pl.pallas_call(
        functools.partial(kernel, (nb, nz, tok, slab, taps, pitch, cp)),
        out_shape=jax.ShapeDtypeStruct((2 * cp, width), BF16),
        in_specs=[any_space] * 5,
        out_specs=pl.BlockSpec(memory_space=pltpu.VMEM),
        scratch_shapes=[
            pltpu.VMEM((2, xn, tok, LANES), BF16),
            pltpu.VMEM((2, xn, tok, LANES), BF16),
            pltpu.VMEM((xn, tok, LANES), BF16),
            pltpu.VMEM((xn, tok, LANES), BF16),
            pltpu.VMEM((xn, tok, LANES), BF16),
            pltpu.VMEM((taps, feats, width), BF16),
            pltpu.VMEM((nb * pitch, LANES), BF16),
            pltpu.VMEM((nb * pitch, 2 * LANES), BF16),
            pltpu.VMEM((2 * pitch, LANES), BF16),
            pltpu.VMEM((pitch, feats), BF16),
            pltpu.VMEM((3, 4 * cp, feats), BF16),
            pltpu.VMEM((2, cp, feats), BF16),
            pltpu.VMEM((tok, feats), BF16),
            dma((xn,)), dma((xn,)), dma((xn,)), dma((xn,)), dma((xn,)), dma((xn,)),
            dma((xn,)), dma((xn,)), dma((xn,)), dma((xn,)), dma((xn,)), dma((xn,)),
            dma((2, half)), dma((2, hops, half)), dma((2, half)), dma((2, hops, half)),
            dma((2,)), dma((2,)), dma((2,)),
        ],
        compiler_params=pltpu.CompilerParams(
            collective_id=0, has_side_effects=True, vmem_limit_bytes=60 * 1024 * 1024),
    )(queries, key_states, value_states, residual, weights)
    return got.reshape(ROWS, cp, width)[:, :COLS].reshape(1, tok, width)


def solution(mesh):
    return jax.shard_map(
        body,
        mesh=mesh,
        in_specs=(
            P(("groups", "batch"), "blk", None),
            P(("groups", "batch"), "blk", None),
            P(("groups", "batch"), "blk", None),
            P(("groups", "batch"), "blk", None),
            P(None, "batch"),
            P(None, None, "batch", None),
        ),
        out_specs=P(("groups", "batch"), "blk", None),
        check_vma=False,
    )
```

time: 211 us -> 111 us (0.53)
  the two profiles are of different devices: /device:TPU:66 before, /device:TPU:65 now
where the time goes in v1:
time: 111 us; the launch traced here: 110 us
  Pallas kernels  106 us (95%)
  local copies, waits for them, and re-layouts  2.59 us (2%)
    pallas_call x1, Pallas kernels, body(): pl.pallas_call(functools.partial(kernel, (nb, nz, tok, slab, taps, pitch,...  106 us

profile of v1, /device:TPU:65, one launch (start us, length us, event | category | flops | bytes accessed | tf_op | source)
XLA Modules:
  0.0 109.5 jit_solution(7395944280568623572)
XLA Ops:
  0.0 0.0 copy-start
  0.0 0.9 pad.4
  1.0 0.1 copy-done
  1.0 0.8 pad_maximum_fusion.w
  1.8 106.1 %shard_map.64 = bf16[160,384]{1,0:T(8,128)(2,1)} custom-call(bf16[1,148,1024]{2,1,0:T(8,128)(2,1)} %q.1, bf16[1,148,1024]{2,1,0:T(8,128)(2,1)} %k.1, bf16[1,148,1024]{2,1,0:T(8,128)(2,1)} %v.1, bf16[1,148,768]{2,1,0:T(8,128)(2,1)} %res.1, bf16[12,48,384]{2,1,0:T(8,128)(2,1)} %pad_maximum_fusion.w), custom_call_target="tpu_custom_call" | custom-call | tf_op jit(solution)/shard_map/pallas_call | solution.py:284
  108.0 1.6 %reshape.15 = bf16[1,148,384]{2,1,0:T(8,128)(2,1)} reshape(bf16[2,74,384]{2,1,0:T(8,128)(2,1)} %bitcast.10) | data formatting | bytes 227328 | tf_op jit(solution)/shard_map/reshape | solution.py:311
  (1 shorter events, 0.0 us)
Async XLA Ops:
  0.0 1.0 copy-start

commit v2 on v1

--- a/solution.py
+++ b/solution.py
@@ -34,12 +34,12 @@
     return jnp.where(ok, 1.0, 0.0).astype(BF16)
 
 
-def kernel(dims, q, k, v, res, w, out, kin, vin, qin, ob, ain, wall, kpad, vaug, qpad,
+def kernel(dims, q, k, v, res, conv, proj, out, kin, vin, qin, ob, ain, wall, kpad, vaug, qpad,
            hpad, grid, hin, rbuf, k_s, k_r, v_s, v_r, q_s, q_r, o_s, o_r, kf_s, kf_r,
-           vf_s, vf_r, w_s, w_r, p_s, p_r, h_s, h_r, loc):
-    nb, nz, tok, slab, taps, pitch, cp = dims
+           vf_s, vf_r, w_s, w_r, p_s, p_r, h_s, h_r, loc, go, flat):
+    nb, nz, tok, slab, taps, pitch, cp, hops = dims
     xn = nb // 2
-    half = taps // 2
+    parts = taps // 3
     blk = lax.axis_index("blk")
     z = lax.axis_index("batch")
     x = blk // 2
@@ -47,7 +47,6 @@
     mate = 2 * x + 1 - c
     side = lax.rem(blk + nb + 2 * c - 1, nb)
     znext = (lax.rem(z + 1, nz), lax.rem(z + nz - 1, nz))
-    hops = (nz // 2, nz - 1 - nz // 2)
 
     def at_x(i):
         off = ((i + 1) // 2) * (2 * (i % 2) - 1)
@@ -63,13 +62,28 @@
         ).start()
 
     barrier = pltpu.get_barrier_semaphore()
-    for i in range(1, xn):
-        pl.semaphore_signal(barrier, inc=1, device_id={"blk": 2 * at_x(i) + c}, device_id_type=MESH)
-    for b in (mate, side):
-        pl.semaphore_signal(barrier, inc=1, device_id={"blk": b}, device_id_type=MESH)
-    for n in znext:
-        pl.semaphore_signal(barrier, inc=1, device_id={"batch": n}, device_id_type=MESH)
-    pl.semaphore_wait(barrier, xn - 1 + 4)
+    for i in range(xn):
+        d = at_x(i)
+        if i > 0:
+            pl.semaphore_signal(barrier, inc=1, device_id={"blk": 2 * d}, device_id_type=MESH)
+        else:
+            @pl.when(c == 1)
+            def _():
+                pl.semaphore_signal(barrier, inc=1, device_id={"blk": mate}, device_id_type=MESH)
+
+    @pl.when(c == 1)
+    def _():
+        for n in znext:
+            pl.semaphore_signal(barrier, inc=1, device_id={"batch": n}, device_id_type=MESH)
+
+    @pl.when(c == 0)
+    def _():
+        pl.semaphore_wait(barrier, nb - 1)
+        pl.semaphore_signal(go, inc=1, device_id={"blk": mate}, device_id_type=MESH)
+
+    @pl.when(c == 1)
+    def _():
+        pl.semaphore_wait(go, 1)
 
     def cols(i):
         return pl.ds(pl.multiple_of(i * LANES, LANES), LANES)
@@ -81,28 +95,46 @@
         d = at_x(i)
         send(k.at[0, :, cols(d)], kin.at[c, x], k_s.at[i], k_r.at[x], blk=2 * d + c)
         send(v.at[0, :, cols(d)], vin.at[c, x], v_s.at[i], v_r.at[x], blk=2 * d + c)
-        if i == 2:
-            for j in range(half):
-                for way in range(2):
-                    send(w.at[half * c + j], wall.at[half * c + j, slab_rows(z)],
-                         w_s.at[way, j], w_r.at[way, 0, j], batch=znext[way])
     for i in range(1, xn):
         d = at_x(i)
         send(q.at[0, :, cols(d)], qin.at[x], q_s.at[i], q_r.at[x], blk=2 * d + c)
     pltpu.make_async_copy(k.at[0, :, cols(x)], kin.at[c, x], k_r.at[x]).start()
     pltpu.make_async_copy(v.at[0, :, cols(x)], vin.at[c, x], v_r.at[x]).start()
     pltpu.make_async_copy(q.at[0, :, cols(x)], qin.at[x], q_r.at[x]).start()
-    pltpu.make_async_copy(w, wall.at[:, slab_rows(z)], loc.at[0]).start()
+    pltpu.make_async_copy(conv, wall.at[0:9, slab_rows(z)], loc.at[0]).start()
     pltpu.make_async_copy(res.at[0], rbuf, loc.at[1]).start()
 
+    def part(j):
+        return pl.ds(3 * lax.rem(j + parts - 1, parts), 3)
+
+    width = wall.shape[2]
+    depth = proj.shape[0]
+    for b in range(taps - 9):
+        n = min(width, depth - b * width)
+        turned = proj[b * width:b * width + n, :].astype(F32).T.astype(BF16)
+        flat[b, :, 0:n] = turned
+        if n < width:
+            flat[b, :, n:width] = jnp.zeros((slab, width - n), BF16)
+        wall[9 + b, slab_rows(z), :] = flat[b]
+
+    @pl.when(c == 1)
+    def _():
+        pl.semaphore_wait(barrier, 2)
+        for j in range(parts):
+            first = 3 * ((j + parts - 1) % parts)
+            src = flat if first == 9 else conv.at[first:first + 3]
+            for way in range(2):
+                send(src, wall.at[part(j), slab_rows(z)], w_s.at[way, j], w_r.at[way, 0, j],
+                     batch=znext[way])
+
     def tick(t, carry):
-        s = t // half
-        j = lax.rem(t, half)
+        s = t // parts
+        j = lax.rem(t, parts)
         for way in range(2):
             zz = lax.rem(z + (1 + s if way else 2 * nz - 1 - s), nz)
 
             def work():
-                ref = wall.at[half * c + j, slab_rows(zz)]
+                ref = wall.at[part(j), slab_rows(zz)]
                 wait(ref, w_r.at[way, s, j])
 
                 @pl.when(s < hops[way] - 1)
@@ -116,14 +148,16 @@
 
                 send(ref, ref, p_s.at[way, j], p_r.at[way, s, j], blk=mate)
 
-            if hops[way] == hops[0]:
+            if hops[way] == max(hops):
                 work()
             else:
                 pl.when(s < hops[way])(work)
         return carry
 
     def ticks(lo, hi):
-        lax.fori_loop(lo, hi, tick, 0)
+        @pl.when(c == 1)
+        def _():
+            lax.fori_loop(lo, hi, tick, 0)
 
     kpad[...] = jnp.zeros_like(kpad)
     vaug[...] = jnp.zeros_like(vaug)
@@ -150,7 +184,7 @@
         wait(vin.at[c, xs], v_r.at[xs])
         send(vin.at[c, xs], vin.at[c, xs], vf_s.at[xs], vf_r.at[xs], blk=mate)
         place(c, xs)
-        lax.fori_loop(2 * i, 2 * i + 2, tick, 0)
+        ticks(i, i + 1)
         return carry
 
     lax.fori_loop(0, xn, take, 0)
@@ -188,25 +222,27 @@
         def _():
             send(ob.at[xs], ain.at[x], o_s.at[xs], o_r.at[x], blk=2 * xs + c)
 
-        lax.fori_loop(2 * xn + 2 * i, 2 * xn + 2 * i + 2, tick, 0)
+        ticks(xn + 2 * i, xn + 2 * i + 2)
         return carry
 
     lax.fori_loop(0, xn, attend, 0)
-    ticks(4 * xn, hops[0] * half)
-
-    for way in range(2):
-        for s in range(hops[way]):
-            zz = lax.rem(z + (1 + s if way else 2 * nz - 1 - s), nz)
-            for j in range(half):
-                wait(wall.at[half * (1 - c) + j, slab_rows(zz)], p_r.at[way, s, j])
-    wait(wall.at[:, slab_rows(z)], loc.at[0])
+    ticks(3 * xn, max(hops) * parts)
+
+    @pl.when(c == 0)
+    def _():
+        for way in range(2):
+            for s in range(hops[way]):
+                zz = lax.rem(z + (1 + s if way else 2 * nz - 1 - s), nz)
+                for j in range(parts):
+                    wait(wall.at[part(j), slab_rows(zz)], p_r.at[way, s, j])
+
+    wait(wall.at[0:9, slab_rows(z)], loc.at[0])
     wait(rbuf, loc.at[1])
     for i in range(1, xn):
         xs = at_x(i)
         wait(ain.at[xs], o_r.at[xs])
 
     attention = jnp.concatenate([ain[i] for i in range(xn)], axis=1)
-    width = wall.shape[2]
     total = rbuf[...].astype(F32)
     convs = taps - (-(-attention.shape[1] // width))
     for b in range(convs, taps):
@@ -253,10 +289,14 @@
     for i in range(xn):
         wait(kin.at[c, i], kf_s.at[i])
         wait(vin.at[c, i], vf_s.at[i])
-    for way in range(2):
-        for j in range(half):
-            wait(wall.at[j, slab_rows(z)], w_s.at[way, j])
-            wait(wall.at[j, slab_rows(z)], p_s.at[way, j])
+
+    @pl.when(c == 1)
+    def _():
+        for way in range(2):
+            for j in range(parts):
+                wait(wall.at[part(j), slab_rows(z)], w_s.at[way, j])
+                wait(wall.at[part(j), slab_rows(z)], p_s.at[way, j])
+
     wait(hin.at[0], h_s.at[0])
     wait(hin.at[1], h_s.at[1])
 
@@ -269,22 +309,21 @@
     width = conv_weight.shape[3]
     depth = proj_weight.shape[0]
     blocks = -(-depth // width)
-    flat = jnp.pad(proj_weight, ((0, blocks * width - depth), (0, 0)))
-    flat = flat.reshape(blocks, width, slab).transpose(0, 2, 1)
-    weights = jnp.concatenate([conv_weight.reshape(9, slab, width), flat], axis=0)
-    taps = weights.shape[0]
-    half = taps // 2
+    taps = 9 + blocks
+    parts = taps // 3
     xn = nb // 2
     pitch = up16(tok)
     cp = up16(COLS)
     feats = nz * slab
-    hops = nz // 2
+    up = (nz - 1) // 3
+    hops = (up, nz - 1 - up)
+    far = max(hops)
     dma = pltpu.SemaphoreType.DMA
     any_space = pl.BlockSpec(memory_space=pl.ANY)
     got = pl.pallas_call(
-        functools.partial(kernel, (nb, nz, tok, slab, taps, pitch, cp)),
+        functools.partial(kernel, (nb, nz, tok, slab, taps, pitch, cp, hops)),
         out_shape=jax.ShapeDtypeStruct((2 * cp, width), BF16),
-        in_specs=[any_space] * 5,
+        in_specs=[any_space] * 5 + [pl.BlockSpec(memory_space=pltpu.VMEM)],
         out_specs=pl.BlockSpec(memory_space=pltpu.VMEM),
         scratch_shapes=[
             pltpu.VMEM((2, xn, tok, LANES), BF16),
@@ -302,12 +341,13 @@
             pltpu.VMEM((tok, feats), BF16),
             dma((xn,)), dma((xn,)), dma((xn,)), dma((xn,)), dma((xn,)), dma((xn,)),
             dma((xn,)), dma((xn,)), dma((xn,)), dma((xn,)), dma((xn,)), dma((xn,)),
-            dma((2, half)), dma((2, hops, half)), dma((2, half)), dma((2, hops, half)),
-            dma((2,)), dma((2,)), dma((2,)),
+            dma((2, parts)), dma((2, far, parts)), dma((2, parts)), dma((2, far, parts)),
+            dma((2,)), dma((2,)), dma((2,)), pltpu.SemaphoreType.REGULAR,
+            pltpu.VMEM((blocks, slab, width), BF16),
         ],
         compiler_params=pltpu.CompilerParams(
             collective_id=0, has_side_effects=True, vmem_limit_bytes=60 * 1024 * 1024),
-    )(queries, key_states, value_states, residual, weights)
+    )(queries, key_states, value_states, residual, conv_weight.reshape(9, slab, width), proj_weight)
     return got.reshape(ROWS, cp, width)[:, :COLS].reshape(1, tok, width)
 
 

time: 111 us -> 116 us (1.045)
  Pallas kernels: 106 us -> 112 us
    pallas_call x1, Pallas kernels: 106 us -> 112 us  [body(): pl.pallas_call(functools.partial(kernel, (nb, nz, tok, slab, taps, pitch,...]
    unnamed x2 -> x1, local copies, waits for them, and re-layouts: 0.05 us -> 1.72 us
where the time goes in v2:
time: 116 us
  Pallas kernels  112 us (97%)
  local copies, waits for them, and re-layouts  3.3 us (3%)
    pallas_call x1, Pallas kernels, body(): pl.pallas_call(functools.partial(kernel, (nb, nz, tok, slab, taps, pitch,...  112 us

profile of v2, /device:TPU:65, one launch (start us, length us, event | category | flops | bytes accessed | tf_op | source)
XLA Modules:
  0.0 115.5 jit_solution(5166119615812139180)
XLA Ops:
  0.0 1.7 %copy.8.proj = bf16[1024,48]{1,0:T(8,128)(2,1)} copy(bf16[1024,48]{0,1:T(8,128)(2,1)} %param.10) | data formatting | bytes 196608 | tf_op args[4]
  1.7 112.2 %shard_map.64 = bf16[160,384]{1,0:T(8,128)(2,1)} custom-call(bf16[1,148,1024]{2,1,0:T(8,128)(2,1)} %q.1, bf16[1,148,1024]{2,1,0:T(8,128)(2,1)} %k.1, bf16[1,148,1024]{2,1,0:T(8,128)(2,1)} %v.1, bf16[1,148,768]{2,1,0:T(8,128)(2,1)} %res.1, bf16[9,48,384]{2,1,0:T(8,128)(2,1)} %bitcast.4, bf16[1024,48]{1,0:T(8,128)(2,1)} %copy.8.proj), custom_call_target="tpu_custom_call" | custom-call | tf_op jit(solution)/shard_map/pallas_call | solution.py:323
  114.0 1.6 %reshape.11 = bf16[1,148,384]{2,1,0:T(8,128)(2,1)} reshape(bf16[2,74,384]{2,1,0:T(8,128)(2,1)} %bitcast.3) | data formatting | bytes 227328 | tf_op jit(solution)/shard_map/reshape | solution.py:351

commit v3 on v2

--- a/solution.py
+++ b/solution.py
@@ -35,8 +35,7 @@
 
 
 def kernel(dims, q, k, v, res, conv, proj, out, kin, vin, qin, ob, ain, wall, kpad, vaug, qpad,
-           hpad, grid, hin, rbuf, k_s, k_r, v_s, v_r, q_s, q_r, o_s, o_r, kf_s, kf_r,
-           vf_s, vf_r, w_s, w_r, p_s, p_r, h_s, h_r, loc, go, flat):
+           hpad, grid, hin, rbuf, k_s, k_r, v_s, v_r, q_s, q_r, o_s, o_r, w_s, w_r, p_s, p_r, h_s, h_r, loc, go, flat, even, odd):
     nb, nz, tok, slab, taps, pitch, cp, hops = dims
     xn = nb // 2
     parts = taps // 3
@@ -93,14 +92,27 @@
 
     for i in range(1, xn):
         d = at_x(i)
-        send(k.at[0, :, cols(d)], kin.at[c, x], k_s.at[i], k_r.at[x], blk=2 * d + c)
-        send(v.at[0, :, cols(d)], vin.at[c, x], v_s.at[i], v_r.at[x], blk=2 * d + c)
-    for i in range(1, xn):
+        send(k.at[0, :, cols(d)], kin.at[c, x], k_s.at[i], k_r.at[c, x], blk=2 * d)
+        send(v.at[0, :, cols(d)], vin.at[c, x], v_s.at[i], v_r.at[c, x], blk=2 * d)
+
+    @pl.when(c == 0)
+    def _():
+        pltpu.make_async_copy(k.at[0, :, cols(x)], kin.at[0, x], k_r.at[0, x]).start()
+        pltpu.make_async_copy(v.at[0, :, cols(x)], vin.at[0, x], v_r.at[0, x]).start()
+        pltpu.make_async_copy(q.at[0, :, cols(x)], qin.at[0, x], q_r.at[0, x]).start()
+
+    @pl.when(c == 1)
+    def _():
+        send(k.at[0, :, cols(x)], kin.at[1, x], k_s.at[0], k_r.at[1, x], blk=mate)
+        send(v.at[0, :, cols(x)], vin.at[1, x], v_s.at[0], v_r.at[1, x], blk=mate)
+        send(q.at[0, :, cols(x)], qin.at[1, x], q_s.at[0], q_r.at[1, x], blk=mate)
+
+    def ask(i):
         d = at_x(i)
-        send(q.at[0, :, cols(d)], qin.at[x], q_s.at[i], q_r.at[x], blk=2 * d + c)
-    pltpu.make_async_copy(k.at[0, :, cols(x)], kin.at[c, x], k_r.at[x]).start()
-    pltpu.make_async_copy(v.at[0, :, cols(x)], vin.at[c, x], v_r.at[x]).start()
-    pltpu.make_async_copy(q.at[0, :, cols(x)], qin.at[x], q_r.at[x]).start()
+        wait(kin.at[0, 0], k_s.at[i])
+        wait(vin.at[0, 0], v_s.at[i])
+        send(q.at[0, :, cols(d)], qin.at[c, x], q_s.at[i], q_r.at[c, x], blk=2 * d)
+
     pltpu.make_async_copy(conv, wall.at[0:9, slab_rows(z)], loc.at[0]).start()
     pltpu.make_async_copy(res.at[0], rbuf, loc.at[1]).start()
 
@@ -127,13 +139,17 @@
                 send(src, wall.at[part(j), slab_rows(z)], w_s.at[way, j], w_r.at[way, 0, j],
                      batch=znext[way])
 
+    lag = 2 * parts
+
     def tick(t, carry):
-        s = t // parts
-        j = lax.rem(t, parts)
         for way in range(2):
+            u = t - (0 if hops[way] == max(hops) else lag)
+            s = u // parts
+            j = u - s * parts
             zz = lax.rem(z + (1 + s if way else 2 * nz - 1 - s), nz)
 
-            def work():
+            @pl.when((u >= 0) & (u < hops[way] * parts))
+            def _():
                 ref = wall.at[part(j), slab_rows(zz)]
                 wait(ref, w_r.at[way, s, j])
 
@@ -148,16 +164,7 @@
 
                 send(ref, ref, p_s.at[way, j], p_r.at[way, s, j], blk=mate)
 
-            if hops[way] == max(hops):
-                work()
-            else:
-                pl.when(s < hops[way])(work)
         return carry
-
-    def ticks(lo, hi):
-        @pl.when(c == 1)
-        def _():
-            lax.fori_loop(lo, hi, tick, 0)
 
     kpad[...] = jnp.zeros_like(kpad)
     vaug[...] = jnp.zeros_like(vaug)
@@ -179,54 +186,75 @@
 
     def take(i, carry):
         xs = at_x(i)
-        wait(kin.at[c, xs], k_r.at[xs])
-        send(kin.at[c, xs], kin.at[c, xs], kf_s.at[xs], kf_r.at[xs], blk=mate)
-        wait(vin.at[c, xs], v_r.at[xs])
-        send(vin.at[c, xs], vin.at[c, xs], vf_s.at[xs], vf_r.at[xs], blk=mate)
-        place(c, xs)
-        ticks(i, i + 1)
+        for p in range(2):
+            wait(kin.at[p, xs], k_r.at[p, xs])
+            wait(vin.at[p, xs], v_r.at[p, xs])
+            place(p, xs)
+
+        @pl.when(i > 0)
+        def _():
+            ask(i)
+
         return carry
-
-    lax.fori_loop(0, xn, take, 0)
-
-    def take_mate(i, carry):
-        xs = at_x(i)
-        wait(kin.at[1 - c, xs], kf_r.at[xs])
-        wait(vin.at[1 - c, xs], vf_r.at[xs])
-        place(1 - c, xs)
-        return carry
-
-    lax.fori_loop(0, xn, take_mate, 0)
 
     lane = lax.broadcasted_iota(jnp.int32, (tok, LANES), 1)
     scale = HD ** -0.5 * LOG2E
 
-    def attend(i, carry):
-        xs = at_x(i)
-        wait(qin.at[xs], q_r.at[xs])
-        qv = qin[xs].astype(F32)
-        qpad[0:tok, :] = jnp.where(lane < HD, qv, 0.0).astype(BF16)
-        qpad[pitch:pitch + tok, :] = jnp.where(lane < HD, 0.0, qv).astype(BF16)
-        scores = lax.dot_general(qpad[...], kpad[...], NT, preferred_element_type=F32)
+    def score(p, xs, held):
+        qv = qin[p, xs].astype(F32)
+        qpad[p, 0:tok, :] = jnp.where(lane < HD, qv, 0.0).astype(BF16)
+        qpad[p, pitch:pitch + tok, :] = jnp.where(lane < HD, 0.0, qv).astype(BF16)
+        held[...] = lax.dot_general(qpad[p], kpad[...], NT, preferred_element_type=F32)
+
+    def mix(p, xs, held):
+        scores = held[...]
         top = jnp.max(scores, axis=1, keepdims=True)
         weights = jnp.exp2((scores - top) * scale).astype(BF16)
         mixed = jnp.dot(weights, vaug[...], preferred_element_type=F32)
         both = mixed[:, :LANES] / mixed[:, LANES:]
-        ob[xs] = jnp.where(lane < HD, both[0:tok], both[pitch:pitch + tok]).astype(BF16)
+        ob[p, xs] = jnp.where(lane < HD, both[0:tok], both[pitch:pitch + tok]).astype(BF16)
+
+    def attend(i, carry):
+        xs = at_x(i)
+        after = at_x(jnp.minimum(i + 1, xn - 1))
+        wait(qin.at[1, xs], q_r.at[1, xs])
+        score(1, xs, odd)
+        mix(0, xs, even)
 
         @pl.when(i == 0)
         def _():
-            ain[x] = ob[x]
+            ain[x] = ob[0, x]
 
         @pl.when(i > 0)
         def _():
-            send(ob.at[xs], ain.at[x], o_s.at[xs], o_r.at[x], blk=2 * xs + c)
-
-        ticks(xn + 2 * i, xn + 2 * i + 2)
+            send(ob.at[0, xs], ain.at[x], o_s.at[0, xs], o_r.at[x], blk=2 * xs)
+
+        @pl.when(i < xn - 1)
+        def _():
+            wait(qin.at[0, after], q_r.at[0, after])
+
+        score(0, after, even)
+        mix(1, xs, odd)
+        send(ob.at[1, xs], ain.at[x], o_s.at[1, xs], o_r.at[x], blk=2 * xs + 1)
         return carry
 
-    lax.fori_loop(0, xn, attend, 0)
-    ticks(3 * xn, max(hops) * parts)
+    @pl.when(c == 0)
+    def _():
+        lax.fori_loop(0, xn, take, 0)
+        wait(qin.at[0, x], q_r.at[0, x])
+        score(0, x, even)
+        lax.fori_loop(0, xn, attend, 0)
+
+    @pl.when(c == 1)
+    def _():
+        def step(i, carry):
+            lax.fori_loop(2 * i - 2, 2 * i, tick, 0)
+            ask(i)
+            return carry
+
+        lax.fori_loop(1, xn, step, 0)
+        last = max(max(hops) * parts, min(hops) * parts + lag)
+        lax.fori_loop(2 * xn - 2, last, tick, 0)
 
     @pl.when(c == 0)
     def _():
@@ -241,6 +269,11 @@
     for i in range(1, xn):
         xs = at_x(i)
         wait(ain.at[xs], o_r.at[xs])
+
+    @pl.when(c == 1)
+    def _():
+        wait(ain.at[x], o_r.at[x])
+
 
     attention = jnp.concatenate([ain[i] for i in range(xn)], axis=1)
     total = rbuf[...].astype(F32)
@@ -281,14 +314,21 @@
     out[cp:2 * cp, :] = lower.astype(BF16)
 
     for i in range(1, xn):
-        xs = at_x(i)
-        wait(kin.at[c, 0], k_s.at[i])
-        wait(vin.at[c, 0], v_s.at[i])
-        wait(qin.at[0], q_s.at[i])
-        wait(ob.at[xs], o_s.at[xs])
-    for i in range(xn):
-        wait(kin.at[c, i], kf_s.at[i])
-        wait(vin.at[c, i], vf_s.at[i])
+        wait(qin.at[0, 0], q_s.at[i])
+
+    @pl.when(c == 0)
+    def _():
+        for i in range(xn):
+            xs = at_x(i)
+            if i > 0:
+                wait(ob.at[0, xs], o_s.at[0, xs])
+            wait(ob.at[1, xs], o_s.at[1, xs])
+
+    @pl.when(c == 1)
+    def _():
+        wait(kin.at[0, 0], k_s.at[0])
+        wait(vin.at[0, 0], v_s.at[0])
+        wait(qin.at[0, 0], q_s.at[0])
 
     @pl.when(c == 1)
     def _():
@@ -315,7 +355,7 @@
     pitch = up16(tok)
     cp = up16(COLS)
     feats = nz * slab
-    up = (nz - 1) // 3
+    up = 2 * (nz - 1) // 5
     hops = (up, nz - 1 - up)
     far = max(hops)
     dma = pltpu.SemaphoreType.DMA
@@ -328,22 +368,24 @@
         scratch_shapes=[
             pltpu.VMEM((2, xn, tok, LANES), BF16),
             pltpu.VMEM((2, xn, tok, LANES), BF16),
-            pltpu.VMEM((xn, tok, LANES), BF16),
-            pltpu.VMEM((xn, tok, LANES), BF16),
+            pltpu.VMEM((2, xn, tok, LANES), BF16),
+            pltpu.VMEM((2, xn, tok, LANES), BF16),
             pltpu.VMEM((xn, tok, LANES), BF16),
             pltpu.VMEM((taps, feats, width), BF16),
             pltpu.VMEM((nb * pitch, LANES), BF16),
             pltpu.VMEM((nb * pitch, 2 * LANES), BF16),
-            pltpu.VMEM((2 * pitch, LANES), BF16),
+            pltpu.VMEM((2, 2 * pitch, LANES), BF16),
             pltpu.VMEM((pitch, feats), BF16),
             pltpu.VMEM((3, 4 * cp, feats), BF16),
             pltpu.VMEM((2, cp, feats), BF16),
             pltpu.VMEM((tok, feats), BF16),
-            dma((xn,)), dma((xn,)), dma((xn,)), dma((xn,)), dma((xn,)), dma((xn,)),
-            dma((xn,)), dma((xn,)), dma((xn,)), dma((xn,)), dma((xn,)), dma((xn,)),
+            dma((xn,)), dma((2, xn)), dma((xn,)), dma((2, xn)), dma((xn,)), dma((2, xn)),
+            dma((2, xn)), dma((xn,)),
             dma((2, parts)), dma((2, far, parts)), dma((2, parts)), dma((2, far, parts)),
             dma((2,)), dma((2,)), dma((2,)), pltpu.SemaphoreType.REGULAR,
             pltpu.VMEM((blocks, slab, width), BF16),
+            pltpu.VMEM((2 * pitch, nb * pitch), F32),
+            pltpu.VMEM((2 * pitch, nb * pitch), F32),
         ],
         compiler_params=pltpu.CompilerParams(
             collective_id=0, has_side_effects=True, vmem_limit_bytes=60 * 1024 * 1024),

time: 116 us -> 100 us (0.86)
  Pallas kernels: 112 us -> 96.5 us
    pallas_call x1, Pallas kernels: 112 us -> 96.5 us  [body(): pl.pallas_call(functools.partial(kernel, (nb, nz, tok, slab, taps, pitch,...]
where the time goes in v3:
time: 100 us; the launch traced here: 99.8 us
  Pallas kernels  96.5 us (96%)
  local copies, waits for them, and re-layouts  3.3 us (3%)
    pallas_call x1, Pallas kernels, body(): pl.pallas_call(functools.partial(kernel, (nb, nz, tok, slab, taps, pitch,...  96.5 us

profile of v3, /device:TPU:65, one launch (start us, length us, event | category | flops | bytes accessed | tf_op | source)
XLA Modules:
  0.0 99.8 jit_solution(6854721164489733280)
XLA Ops:
  0.0 1.7 %copy.8.proj = bf16[1024,48]{1,0:T(8,128)(2,1)} copy(bf16[1024,48]{0,1:T(8,128)(2,1)} %param.10) | data formatting | bytes 196608 | tf_op args[4]
  1.7 96.5 %shard_map.64 = bf16[160,384]{1,0:T(8,128)(2,1)} custom-call(bf16[1,148,1024]{2,1,0:T(8,128)(2,1)} %q.1, bf16[1,148,1024]{2,1,0:T(8,128)(2,1)} %k.1, bf16[1,148,1024]{2,1,0:T(8,128)(2,1)} %v.1, bf16[1,148,768]{2,1,0:T(8,128)(2,1)} %res.1, bf16[9,48,384]{2,1,0:T(8,128)(2,1)} %bitcast.4, bf16[1024,48]{1,0:T(8,128)(2,1)} %copy.8.proj), custom_call_target="tpu_custom_call" | custom-call | tf_op jit(solution)/shard_map/pallas_call | solution.py:363
  98.2 1.6 %reshape.11 = bf16[1,148,384]{2,1,0:T(8,128)(2,1)} reshape(bf16[2,74,384]{2,1,0:T(8,128)(2,1)} %bitcast.3) | data formatting | bytes 227328 | tf_op jit(solution)/shard_map/reshape | solution.py:393

commit v4 on v3

--- a/solution.py
+++ b/solution.py
@@ -35,12 +35,14 @@
 
 
 def kernel(dims, q, k, v, res, conv, proj, out, kin, vin, qin, ob, ain, wall, kpad, vaug, qpad,
-           hpad, grid, hin, rbuf, k_s, k_r, v_s, v_r, q_s, q_r, o_s, o_r, w_s, w_r, p_s, p_r, h_s, h_r, loc, go, flat, even, odd):
+           hpad, grid, hin, rbuf, k_s, k_r, v_s, v_r, q_s, q_r, o_s, o_r, w_s, w_r, p_s, p_r, h_s, h_r, loc, go, flat, even, odd, y_s, y_r):
     nb, nz, tok, slab, taps, pitch, cp, hops = dims
     xn = nb // 2
     parts = taps // 3
     blk = lax.axis_index("blk")
     z = lax.axis_index("batch")
+    g = lax.axis_index("groups")
+    other = g + 1 - 2 * (g % 2)
     x = blk // 2
     c = blk % 2
     mate = 2 * x + 1 - c
@@ -74,6 +76,7 @@
     def _():
         for n in znext:
             pl.semaphore_signal(barrier, inc=1, device_id={"batch": n}, device_id_type=MESH)
+        pl.semaphore_signal(barrier, inc=1, device_id={"groups": other}, device_id_type=MESH)
 
     @pl.when(c == 0)
     def _():
@@ -117,7 +120,10 @@
     pltpu.make_async_copy(res.at[0], rbuf, loc.at[1]).start()
 
     def part(j):
-        return pl.ds(3 * lax.rem(j + parts - 1, parts), 3)
+        mine, theirs = 3 + 3 * (g % 2), 6 - 3 * (g % 2)
+        if isinstance(j, int):
+            return pl.ds((9, 0, mine, theirs)[j], 3)
+        return pl.ds(jnp.where(j == 0, 9, jnp.where(j == 1, 0, jnp.where(j == 2, mine, theirs))), 3)
 
     width = wall.shape[2]
     depth = proj.shape[0]
@@ -131,15 +137,25 @@
 
     @pl.when(c == 1)
     def _():
-        pl.semaphore_wait(barrier, 2)
-        for j in range(parts):
-            first = 3 * ((j + parts - 1) % parts)
-            src = flat if first == 9 else conv.at[first:first + 3]
+        pl.semaphore_wait(barrier, 3)
+        for j in range(parts - 1):
+            src = flat if j == 0 else conv.at[part(j)]
             for way in range(2):
                 send(src, wall.at[part(j), slab_rows(z)], w_s.at[way, j], w_r.at[way, 0, j],
                      batch=znext[way])
 
     lag = 2 * parts
+
+    def hand(way, s):
+        zz = lax.rem(z + (1 + s if way else 2 * nz - 1 - s), nz)
+        ref = wall.at[part(parts - 1), slab_rows(zz)]
+        wait(ref, y_r.at[way, s])
+
+        @pl.when(s > 0)
+        def _():
+            wait(ref, p_s.at[way, parts - 1])
+
+        send(ref, ref, p_s.at[way, parts - 1], p_r.at[way, s, parts - 1], blk=mate)
 
     def tick(t, carry):
         for way in range(2):
@@ -148,7 +164,9 @@
             j = u - s * parts
             zz = lax.rem(z + (1 + s if way else 2 * nz - 1 - s), nz)
 
-            @pl.when((u >= 0) & (u < hops[way] * parts))
+            inside = (u >= 0) & (u < hops[way] * parts)
+
+            @pl.when(inside & (j < parts - 1))
             def _():
                 ref = wall.at[part(j), slab_rows(zz)]
                 wait(ref, w_r.at[way, s, j])
@@ -158,11 +176,23 @@
                     wait(ref, w_s.at[way, j])
                     send(ref, ref, w_s.at[way, j], w_r.at[way, s + 1, j], batch=znext[way])
 
+                @pl.when(j == parts - 2)
+                def _():
+                    @pl.when(s > 0)
+                    def _():
+                        wait(ref, y_s.at[way])
+
+                    send(ref, ref, y_s.at[way], y_r.at[way, s], groups=other)
+
                 @pl.when(s > 0)
                 def _():
                     wait(ref, p_s.at[way, j])
 
                 send(ref, ref, p_s.at[way, j], p_r.at[way, s, j], blk=mate)
+
+            @pl.when(inside & (j == parts - 1) & (s > 0))
+            def _():
+                hand(way, s - 1)
 
         return carry
 
@@ -200,17 +230,26 @@
     lane = lax.broadcasted_iota(jnp.int32, (tok, LANES), 1)
     scale = HD ** -0.5 * LOG2E
 
-    def score(p, xs, held):
+    keys = kpad.shape[0]
+    piece = keys // 5
+
+    def spread(p, xs):
         qv = qin[p, xs].astype(F32)
         qpad[p, 0:tok, :] = jnp.where(lane < HD, qv, 0.0).astype(BF16)
         qpad[p, pitch:pitch + tok, :] = jnp.where(lane < HD, 0.0, qv).astype(BF16)
-        held[...] = lax.dot_general(qpad[p], kpad[...], NT, preferred_element_type=F32)
-
-    def mix(p, xs, held):
-        scores = held[...]
-        top = jnp.max(scores, axis=1, keepdims=True)
-        weights = jnp.exp2((scores - top) * scale).astype(BF16)
-        mixed = jnp.dot(weights, vaug[...], preferred_element_type=F32)
+
+    def score(p, held, lo):
+        held[:, lo:lo + piece] = lax.dot_general(
+            qpad[p], kpad[lo:lo + piece, :], NT, preferred_element_type=F32)
+
+    def work(p, xs, held, p_next, xs_next, held_next):
+        spread(p_next, xs_next)
+        top = jnp.max(held[...], axis=1, keepdims=True)
+        mixed = jnp.zeros((2 * pitch, 2 * LANES), F32)
+        for lo in range(0, keys, piece):
+            score(p_next, held_next, lo)
+            weights = jnp.exp2((held[:, lo:lo + piece] - top) * scale).astype(BF16)
+            mixed += jnp.dot(weights, vaug[lo:lo + piece, :], preferred_element_type=F32)
         both = mixed[:, :LANES] / mixed[:, LANES:]
         ob[p, xs] = jnp.where(lane < HD, both[0:tok], both[pitch:pitch + tok]).astype(BF16)
 
@@ -218,8 +257,7 @@
         xs = at_x(i)
         after = at_x(jnp.minimum(i + 1, xn - 1))
         wait(qin.at[1, xs], q_r.at[1, xs])
-        score(1, xs, odd)
-        mix(0, xs, even)
+        work(0, xs, even, 1, xs, odd)
 
         @pl.when(i == 0)
         def _():
@@ -233,8 +271,7 @@
         def _():
             wait(qin.at[0, after], q_r.at[0, after])
 
-        score(0, after, even)
-        mix(1, xs, odd)
+        work(1, xs, odd, 0, after, even)
         send(ob.at[1, xs], ain.at[x], o_s.at[1, xs], o_r.at[x], blk=2 * xs + 1)
         return carry
 
@@ -242,7 +279,9 @@
     def _():
         lax.fori_loop(0, xn, take, 0)
         wait(qin.at[0, x], q_r.at[0, x])
-        score(0, x, even)
+        spread(0, x)
+        for lo in range(0, keys, piece):
+            score(0, even, lo)
         lax.fori_loop(0, xn, attend, 0)
 
     @pl.when(c == 1)
@@ -255,6 +294,8 @@
         lax.fori_loop(1, xn, step, 0)
         last = max(max(hops) * parts, min(hops) * parts + lag)
         lax.fori_loop(2 * xn - 2, last, tick, 0)
+        for way in range(2):
+            hand(way, jnp.int32(hops[way] - 1))
 
     @pl.when(c == 0)
     def _():
@@ -333,8 +374,10 @@
     @pl.when(c == 1)
     def _():
         for way in range(2):
+            wait(wall.at[part(0), slab_rows(z)], y_s.at[way])
             for j in range(parts):
-                wait(wall.at[part(j), slab_rows(z)], w_s.at[way, j])
+                if j < parts - 1:
+                    wait(wall.at[part(j), slab_rows(z)], w_s.at[way, j])
                 wait(wall.at[part(j), slab_rows(z)], p_s.at[way, j])
 
     wait(hin.at[0], h_s.at[0])
@@ -386,6 +429,7 @@
             pltpu.VMEM((blocks, slab, width), BF16),
             pltpu.VMEM((2 * pitch, nb * pitch), F32),
             pltpu.VMEM((2 * pitch, nb * pitch), F32),
+            dma((2,)), dma((2, far)),
         ],
         compiler_params=pltpu.CompilerParams(
             collective_id=0, has_side_effects=True, vmem_limit_bytes=60 * 1024 * 1024),

time: 100 us -> 99.1 us (level)
  no operation moved by 1% of the time
where the time goes in v4:
time: 99.1 us; the launch traced here: 98.9 us
  Pallas kernels  95.6 us (96%)
  local copies, waits for them, and re-layouts  3.3 us (3%)
    pallas_call x1, Pallas kernels, body(): pl.pallas_call(functools.partial(kernel, (nb, nz, tok, slab, taps, pitch,...  95.6 us

profile of v4, /device:TPU:65, one launch (start us, length us, event | category | flops | bytes accessed | tf_op | source)
XLA Modules:
  0.0 98.9 jit_solution(13884123382180163887)
XLA Ops:
  0.0 1.7 %copy.8.proj = bf16[1024,48]{1,0:T(8,128)(2,1)} copy(bf16[1024,48]{0,1:T(8,128)(2,1)} %param.10) | data formatting | bytes 196608 | tf_op args[4]
  1.7 95.6 %shard_map.64 = bf16[160,384]{1,0:T(8,128)(2,1)} custom-call(bf16[1,148,1024]{2,1,0:T(8,128)(2,1)} %q.1, bf16[1,148,1024]{2,1,0:T(8,128)(2,1)} %k.1, bf16[1,148,1024]{2,1,0:T(8,128)(2,1)} %v.1, bf16[1,148,768]{2,1,0:T(8,128)(2,1)} %res.1, bf16[9,48,384]{2,1,0:T(8,128)(2,1)} %bitcast.4, bf16[1024,48]{1,0:T(8,128)(2,1)} %copy.8.proj), custom_call_target="tpu_custom_call" | custom-call | tf_op jit(solution)/shard_map/pallas_call | solution.py:406
  97.3 1.6 %reshape.11 = bf16[1,148,384]{2,1,0:T(8,128)(2,1)} reshape(bf16[2,74,384]{2,1,0:T(8,128)(2,1)} %bitcast.3) | data formatting | bytes 227328 | tf_op jit(solution)/shard_map/reshape | solution.py:437

commit v5 on v4

--- a/solution.py
+++ b/solution.py
@@ -287,13 +287,13 @@
     @pl.when(c == 1)
     def _():
         def step(i, carry):
-            lax.fori_loop(2 * i - 2, 2 * i, tick, 0)
+            lax.fori_loop(3 * i - 3, 3 * i, tick, 0)
             ask(i)
             return carry
 
         lax.fori_loop(1, xn, step, 0)
         last = max(max(hops) * parts, min(hops) * parts + lag)
-        lax.fori_loop(2 * xn - 2, last, tick, 0)
+        lax.fori_loop(3 * xn - 3, last, tick, 0)
         for way in range(2):
             hand(way, jnp.int32(hops[way] - 1))
 

time: 99.1 us -> 99.2 us (level)
  no operation moved by 1% of the time
where the time goes in v5:
time: 99.2 us; the launch traced here: 98.9 us
  Pallas kernels  95.6 us (96%)
  local copies, waits for them, and re-layouts  3.3 us (3%)
    pallas_call x1, Pallas kernels, body(): pl.pallas_call(functools.partial(kernel, (nb, nz, tok, slab, taps, pitch,...  95.6 us

profile of v5, /device:TPU:65, one launch (start us, length us, event | category | flops | bytes accessed | tf_op | source)
XLA Modules:
  0.0 98.9 jit_solution(10447784288529694380)
XLA Ops:
  0.0 1.7 %copy.8.proj = bf16[1024,48]{1,0:T(8,128)(2,1)} copy(bf16[1024,48]{0,1:T(8,128)(2,1)} %param.10) | data formatting | bytes 196608 | tf_op args[4]
  1.7 95.6 %shard_map.64 = bf16[160,384]{1,0:T(8,128)(2,1)} custom-call(bf16[1,148,1024]{2,1,0:T(8,128)(2,1)} %q.1, bf16[1,148,1024]{2,1,0:T(8,128)(2,1)} %k.1, bf16[1,148,1024]{2,1,0:T(8,128)(2,1)} %v.1, bf16[1,148,768]{2,1,0:T(8,128)(2,1)} %res.1, bf16[9,48,384]{2,1,0:T(8,128)(2,1)} %bitcast.4, bf16[1024,48]{1,0:T(8,128)(2,1)} %copy.8.proj), custom_call_target="tpu_custom_call" | custom-call | tf_op jit(solution)/shard_map/pallas_call | solution.py:406
  97.4 1.6 %reshape.11 = bf16[1,148,384]{2,1,0:T(8,128)(2,1)} reshape(bf16[2,74,384]{2,1,0:T(8,128)(2,1)} %bitcast.3) | data formatting | bytes 227328 | tf_op jit(solution)/shard_map/reshape | solution.py:437
